TPU v7x, 32 devices: a whole 2x2x4 slice. The times are simulated.
32 devices in a mesh: doc: 2 (over x), seq: 4 (over y, core), head: 4 (over z).
Axes of the slice: x: 2, y: 2, z: 4, core: 2. Of those that a mesh axis runs over, the one named last changes fastest.
Arguments:
- length: int32 [2], P('doc'), parts along dimension 0, may hold values from 896 to 1024
- residual: bfloat16 [2048, 4096], P(('doc', 'seq'), 'head'), parts along dimension 0, may hold values from -6 to 6
- ssm_input: bfloat16 [2048, 4096], P(('doc', 'seq'), 'head'), parts along dimension 0, may hold values from -6 to 6
- state_in: bfloat16 [2048, 128], P(('doc', 'seq')), parts along dimension 0, may hold values from -6 to 6
- state_out: bfloat16 [2048, 128], P(('doc', 'seq')), parts along dimension 0, may hold values from -0.5 to 0.5
- step_raw: float32 [128, 1024], P(('doc', 'head'), 'seq'), parts along dimension 0, may hold values from -5 to 2
- decay_rate: float32 [64], P('head'), may hold values from 0 to 1, as said below
- ssm_gain: float32 [4096], P('head'), may hold values from 0.1 to 1.9
- out_weight: bfloat16 [4096, 4096], P('head'), may hold values from -0.09375 to 0.09375
- norm_gain: float32 [4096], replicated, may hold values from 0.1 to 1.9
- query_weight: bfloat16 [4096, 4096], P(None, 'head'), may hold values from -2 to 2
- key_weight: bfloat16 [4096, 1024], P(None, 'head'), may hold values from -3 to 3
- value_weight: bfloat16 [4096, 1024], P(None, 'head'), may hold values from -0.09375 to 0.09375
Outputs:
- layer_out: bfloat16 [2048, 4096], P(('doc', 'seq'), 'head'), parts along dimension 0
- head_out: bfloat16 [2048, 4096], P(('doc', 'seq'), 'head'), parts along dimension 0
There are 2 independent parts, one for each index of `doc`. A program takes and returns all parts, laid end to end along the dimension named above; an argument that names none is the same for every part. Nothing has to cross between parts.
Inputs may be any that keep to these rules, and one draw needn't show every extreme that they name: The document fills positions 0 to length - 1 of the 1024; later positions are padding. `decay_rate`: positive.
All inputs are finite; a program needn't handle non-finite values.
Results may differ from a plain program's by a relative error of at most 0.028.
The roundings to bfloat16 on the way count: a program that leaves them out, or rounds other values in their place, can miss the bound.
Values may be sent and summed in bfloat16 or wider, within the bound.
A program may use at most 64 MiB of HBM per device.

v0:
```python
import functools

import jax
import jax.numpy as jnp
from jax import lax
from jax.experimental import pallas as pl
from jax.experimental.pallas import tpu as pltpu
from jax.sharding import PartitionSpec as P

HEAD_DIM = 128


EPSILON = 1e-05
NEG_BIG = -1e30
HIGHEST = lax.Precision.HIGHEST


def chain_kernel(
    count, chunks, decay_ref, state_ref, incoming_ref, stage_ref, landed_ref, send_sem, recv_sem
):
    mine = lax.axis_index("seq")
    last = count - 1
    heads = state_ref.shape[0] // chunks
    barrier = pltpu.get_barrier_semaphore()

    def greet(neighbour):
        pl.semaphore_signal(
            barrier, inc=1, device_id={"seq": neighbour}, device_id_type=pl.DeviceIdType.MESH
        )

    @pl.when(mine > 0)
    def _():
        greet(mine - 1)

    @pl.when(mine < last)
    def _():
        greet(mine + 1)

    @pl.when((mine == 0) | (mine == last))
    def _():
        pl.semaphore_wait(barrier, 1)

    @pl.when((mine > 0) & (mine < last))
    def _():
        pl.semaphore_wait(barrier, 2)

    def copy(chunk):
        return pltpu.make_async_remote_copy(
            src_ref=stage_ref.at[chunk],
            dst_ref=landed_ref.at[chunk],
            send_sem=send_sem.at[chunk],
            recv_sem=recv_sem.at[chunk],
            device_id={"seq": mine + 1},
            device_id_type=pl.DeviceIdType.MESH,
        )

    for chunk in range(chunks):
        here = pl.ds(chunk * heads, heads)

        @pl.when(mine == 0)
        def _():
            incoming_ref[here] = jnp.zeros((heads,) + state_ref.shape[1:], jnp.float32)

        @pl.when(mine > 0)
        def _():
            copy(chunk).wait_recv()
            incoming_ref[here] = landed_ref[chunk].astype(jnp.float32)

        @pl.when(mine < last)
        def _():
            for index in range(heads):
                head = chunk * heads + index
                outgoing = decay_ref[head] * incoming_ref[head] + state_ref[head]
                stage_ref[chunk, index] = outgoing.astype(jnp.bfloat16)
            copy(chunk).start()

    for chunk in range(chunks):

        @pl.when(mine < last)
        def _():
            copy(chunk).wait_send()


def incoming_state(block_decay, local_state, count):
    heads, width, states = local_state.shape
    chunks = 4 if heads % 4 == 0 else 1
    slots = (chunks, heads // chunks, width, states)
    return pl.pallas_call(
        functools.partial(chain_kernel, count, chunks),
        out_shape=jax.ShapeDtypeStruct(local_state.shape, jnp.float32),
        in_specs=[
            pl.BlockSpec(memory_space=pltpu.SMEM),
            pl.BlockSpec(memory_space=pltpu.VMEM),
        ],
        out_specs=pl.BlockSpec(memory_space=pltpu.VMEM),
        scratch_shapes=[
            pltpu.VMEM(slots, jnp.bfloat16),
            pltpu.VMEM(slots, jnp.bfloat16),
            pltpu.SemaphoreType.DMA((chunks,)),
            pltpu.SemaphoreType.DMA((chunks,)),
        ],
        compiler_params=pltpu.CompilerParams(collective_id=1, has_side_effects=True),
    )(block_decay, local_state)


def line_kernel(
    count,
    shards,
    chunks,
    normed_ref,
    out_weight_ref,
    residual_ref,
    gain_ref,
    query_weight_ref,
    key_weight_ref,
    value_weight_ref,
    layer_ref,
    query_ref,
    key_value_ref,
    block_weight_ref,
    partial_ref,
    weight_ref,
    attn_ref,
    shared_ref,
    stage_ref,
    landed_ref,
    gathered_ref,
    total_ref,
    sum_send,
    sum_recv,
    copy_send,
    copy_recv,
    shard_send,
    shard_recv,
    weight_sem,
    block_sem,
):
    mine = lax.axis_index("head")
    last = count - 1
    width = residual_ref.shape[1]
    rows = residual_ref.shape[0] // chunks
    place = (mine, last - mine)

    shard = lax.axis_index("seq")
    query_width = query_ref.shape[1]
    kv_width = key_weight_ref.shape[1]
    starts = (0, kv_width, 2 * kv_width)
    loads = [
        pltpu.make_async_copy(
            source, weight_ref.at[:, pl.ds(start, source.shape[1])], weight_sem.at[index]
        )
        for index, (source, start) in enumerate(
            zip((key_weight_ref, value_weight_ref, query_weight_ref), starts)
        )
    ]

    def ordered(index):
        return jnp.where(2 * mine < count, last - index, index)

    def block_load(index):
        columns = pl.ds(pl.multiple_of(ordered(index) * width, 128), width)
        return pltpu.make_async_copy(
            out_weight_ref.at[:, columns], block_weight_ref.at[index], block_sem.at[index]
        )

    for index in range(count):
        block_load(index).start()
    for load in loads:
        load.start()

    def compute_block(index):
        block_load(index).wait()
        tile = min(width, 256)

        @pl.loop(0, width // tile)
        def _(step):
            columns = pl.ds(pl.multiple_of(step * tile, 128), tile)
            partial_ref[ordered(index), :, columns] = jnp.dot(
                normed_ref[...],
                block_weight_ref[index, :, columns],
                preferred_element_type=jnp.float32,
            )

    barrier = pltpu.get_barrier_semaphore()

    def greet(neighbour):
        pl.semaphore_signal(
            barrier, inc=1, device_id={"head": neighbour}, device_id_type=pl.DeviceIdType.MESH
        )

    @pl.when(mine > 0)
    def _():
        greet(mine - 1)

    @pl.when(mine < last)
    def _():
        greet(mine + 1)

    for offset in range(1, shards):
        other = (shard + offset) % shards
        pl.semaphore_signal(
            barrier, inc=1, device_id={"seq": other}, device_id_type=pl.DeviceIdType.MESH
        )

    @pl.when((mine == 0) | (mine == last))
    def _():
        pl.semaphore_wait(barrier, shards)

    @pl.when((mine > 0) & (mine < last))
    def _():
        pl.semaphore_wait(barrier, shards + 1)

    for other in range(shards):

        @pl.when(other > shard)
        def _():
            shared_ref[pl.ds(other * residual_ref.shape[0], residual_ref.shape[0])] = jnp.zeros(
                (residual_ref.shape[0], 2 * kv_width), jnp.bfloat16
            )

    def neighbour(way):
        return mine + 1 if way == 0 else mine - 1

    def real(way, position):
        return position if way == 0 else last - position

    def sum_copy(way, chunk, step):
        return pltpu.make_async_remote_copy(
            src_ref=stage_ref.at[way, chunk, step],
            dst_ref=landed_ref.at[way, chunk, step],
            send_sem=sum_send.at[way, chunk, step],
            recv_sem=sum_recv.at[way, chunk, step],
            device_id={"head": neighbour(way)},
            device_id_type=pl.DeviceIdType.MESH,
        )

    def block_copy(way, chunk, step, source):
        block = gathered_ref.at[source, pl.ds(chunk * rows, rows)]
        return pltpu.make_async_remote_copy(
            src_ref=block,
            dst_ref=block,
            send_sem=copy_send.at[way, chunk, step],
            recv_sem=copy_recv.at[way, chunk, step],
            device_id={"head": neighbour(way)},
            device_id_type=pl.DeviceIdType.MESH,
        )

    def shard_copy(chunk, offset, source):
        start = pl.multiple_of(source * residual_ref.shape[0] + chunk * rows, 16)
        block = shared_ref.at[pl.ds(start, rows)]
        return pltpu.make_async_remote_copy(
            src_ref=block,
            dst_ref=block,
            send_sem=shard_send.at[chunk, offset],
            recv_sem=shard_recv.at[chunk, offset],
            device_id={"seq": (shard + offset) % shards},
            device_id_type=pl.DeviceIdType.MESH,
        )

    def project(chunk):
        here = pl.ds(chunk * rows, rows)
        there = pl.ds(pl.multiple_of(shard * residual_ref.shape[0] + chunk * rows, 16), rows)

        def product(tile):
            columns = pl.ds(pl.multiple_of(tile * kv_width, 128), kv_width)
            return jnp.dot(
                attn_ref[here], weight_ref[:, columns], preferred_element_type=jnp.float32
            ).astype(jnp.bfloat16)

        if chunk == 0:
            for load in loads:
                load.wait()

        @pl.loop(0, 2)
        def _(tile):
            columns = pl.ds(pl.multiple_of(tile * kv_width, 128), kv_width)
            shared_ref[there, columns] = product(tile)

        for offset in range(1, shards):

            @pl.when(shard + offset < shards)
            def _():
                shard_copy(chunk, offset, shard).start()

        @pl.loop(0, query_width // kv_width)
        def _(tile):
            columns = pl.ds(pl.multiple_of(tile * kv_width, 128), kv_width)
            query_ref[here, columns] = product(tile + 2)

    def own_part(chunk, owner):
        return partial_ref[owner, pl.ds(chunk * rows, rows)]

    def sum_step(chunk, step):
        for way in range(2):
            owner = real(way, last - step + place[way])

            @pl.when(place[way] == 0)
            def _():
                stage_ref[way, chunk, step] = own_part(chunk, owner).astype(jnp.bfloat16)
                sum_copy(way, chunk, step).start()

            if step == 0:
                continue

            @pl.when((place[way] <= step) & (place[way] > 0))
            def _():
                sum_copy(way, chunk, step - 1).wait_recv()
                arrived = landed_ref[way, chunk, step - 1].astype(jnp.float32)
                stage_ref[way, chunk, step] = (own_part(chunk, owner) + arrived).astype(
                    jnp.bfloat16
                )
                sum_copy(way, chunk, step).start()

    def finish_sum(chunk):
        here = pl.ds(chunk * rows, rows)
        total_ref[...] = residual_ref[here].astype(jnp.float32) + own_part(chunk, mine)
        for way in range(2):

            @pl.when(place[way] > 0)
            def _():
                sum_copy(way, chunk, last - 1).wait_recv()
                total_ref[...] += landed_ref[way, chunk, last - 1].astype(jnp.float32)

        layer_low = total_ref[...].astype(jnp.bfloat16)
        gathered_ref[mine, here] = layer_low
        layer_ref[here] = layer_low
        for way in range(2):

            @pl.when(place[way] < last)
            def _():
                block_copy(way, chunk, 0, mine).start()

    def forward(chunk, step):
        for way in range(2):
            source = real(way, place[way] - step)

            @pl.when(place[way] >= step)
            def _():
                block_copy(way, chunk, step - 1, source).wait_recv()

            @pl.when((place[way] >= step) & (place[way] < last))
            def _():
                block_copy(way, chunk, step, source).start()

    def normalise(chunk):
        for way in range(2):

            @pl.when(place[way] == last)
            def _():
                block_copy(way, chunk, last - 1, real(way, 0)).wait_recv()

        here = pl.ds(chunk * rows, rows)
        squares = jnp.zeros((rows, 1), jnp.float32)
        for source in range(count):
            block = gathered_ref[source, here].astype(jnp.float32)
            squares += jnp.sum(block * block, axis=1, keepdims=True)
        scale = lax.rsqrt(squares / (count * width) + EPSILON)
        for source in range(count):
            columns = slice(source * width, (source + 1) * width)
            block = gathered_ref[source, here].astype(jnp.float32)
            attn_ref[here, columns] = (block * scale * gain_ref[:, columns]).astype(jnp.bfloat16)

    for tick in range(chunks + 2 * last):
        for index in range(count) if tick < 3 else ():
            if min(index, 2) == tick:
                compute_block(index)
        for chunk in range(chunks):
            stage = tick - chunk
            if 0 <= stage < last:
                sum_step(chunk, stage)
            elif stage == last:
                finish_sum(chunk)
            elif last < stage < 2 * last:
                forward(chunk, stage - last)
        if 0 <= tick - 2 * last < chunks:
            normalise(tick - 2 * last)
            project(tick - 2 * last)

    for chunk in range(chunks):
        for step in range(last):
            for way in range(2):

                @pl.when(place[way] <= step)
                def _():
                    sum_copy(way, chunk, step).wait_send()

                @pl.when((place[way] >= step) & (place[way] < last))
                def _():
                    block_copy(way, chunk, step, real(way, place[way] - step)).wait_send()

        for offset in range(1, shards):

            @pl.when(shard + offset < shards)
            def _():
                shard_copy(chunk, offset, shard).wait_send()

            @pl.when(shard >= offset)
            def _():
                shard_copy(chunk, offset, shard - offset).wait_recv()

    key_value_ref[...] = shared_ref[...]


def line_layer(normed, out_weight, residual, norm_gain, weights, count, shards):
    rows, width = residual.shape
    model_width = width * count
    query_width, kv_width = weights[0].shape[1], weights[1].shape[1]
    chunks = 4 if rows % 64 == 0 else 1
    piece = rows // chunks
    messages = (2, chunks, count - 1)
    vmem = pl.BlockSpec(memory_space=pltpu.VMEM)
    hbm = pl.BlockSpec(memory_space=pltpu.HBM)
    return pl.pallas_call(
        functools.partial(line_kernel, count, shards, chunks),
        out_shape=(
            jax.ShapeDtypeStruct((rows, width), jnp.bfloat16),
            jax.ShapeDtypeStruct((rows, query_width), jnp.bfloat16),
            jax.ShapeDtypeStruct((shards * rows, 2 * kv_width), jnp.bfloat16),
        ),
        in_specs=[vmem, hbm, vmem, vmem, hbm, hbm, hbm],
        out_specs=[vmem] * 3,
        scratch_shapes=[
            pltpu.VMEM((count, out_weight.shape[0], width), jnp.bfloat16),
            pltpu.VMEM((count, rows, width), jnp.float32),
            pltpu.VMEM((model_width, 2 * kv_width + query_width), jnp.bfloat16),
            pltpu.VMEM((rows, model_width), jnp.bfloat16),
            pltpu.VMEM((shards * rows, 2 * kv_width), jnp.bfloat16),
            pltpu.VMEM(messages + (piece, width), jnp.bfloat16),
            pltpu.VMEM(messages + (piece, width), jnp.bfloat16),
            pltpu.VMEM((count, rows, width), jnp.bfloat16),
            pltpu.VMEM((piece, width), jnp.float32),
            pltpu.SemaphoreType.DMA(messages),
            pltpu.SemaphoreType.DMA(messages),
            pltpu.SemaphoreType.DMA(messages),
            pltpu.SemaphoreType.DMA(messages),
            pltpu.SemaphoreType.DMA((chunks, shards)),
            pltpu.SemaphoreType.DMA((chunks, shards)),
            pltpu.SemaphoreType.DMA((3,)),
            pltpu.SemaphoreType.DMA((count,)),
        ],
        compiler_params=pltpu.CompilerParams(
            collective_id=0, has_side_effects=True, vmem_limit_bytes=52 * 1024 * 1024
        ),
    )(normed, out_weight, residual, norm_gain.reshape(1, model_width), *weights)


def attention_kernel(group_size, limits_ref, query_ref, key_ref, value_ref, out_ref):
    rows, count = query_ref.shape[0], key_ref.shape[0]
    limit, first = limits_ref[0], limits_ref[1]
    key_pos = lax.broadcasted_iota(jnp.int32, (rows, count), 1)
    positions = first + lax.broadcasted_iota(jnp.int32, (rows, count), 0)
    allowed = (key_pos <= positions) & (key_pos < limit)
    live = first + lax.broadcasted_iota(jnp.int32, (rows, 1), 0) < limit
    for head in range(group_size):
        columns = slice(head * HEAD_DIM, (head + 1) * HEAD_DIM)
        scores = lax.dot_general(
            query_ref[:, columns],
            key_ref[...],
            (((1,), (1,)), ((), ())),
            preferred_element_type=jnp.float32,
        ) * HEAD_DIM ** (-0.5)
        masked = jnp.where(allowed, scores, NEG_BIG)
        weights = jnp.exp(masked - jnp.max(masked, axis=1, keepdims=True))
        total = jnp.sum(weights, axis=1, keepdims=True)
        accum = jnp.dot(
            weights.astype(jnp.bfloat16), value_ref[...], preferred_element_type=jnp.float32
        )
        head_out = jnp.where(live, accum / jnp.where(live, total, 1.0), 0.0)
        out_ref[:, columns] = head_out.astype(jnp.bfloat16)


def attention(queries, key_value, limit, first):
    rows, count = queries.shape[0], key_value.shape[0]
    kv_local = key_value.shape[1] // (2 * HEAD_DIM)
    group_size = queries.shape[1] // (kv_local * HEAD_DIM)
    wide = (rows, group_size * HEAD_DIM)
    return pl.pallas_call(
        functools.partial(attention_kernel, group_size),
        grid=(kv_local,),
        out_shape=jax.ShapeDtypeStruct(queries.shape, jnp.bfloat16),
        in_specs=[
            pl.BlockSpec(memory_space=pltpu.SMEM),
            pl.BlockSpec(wide, lambda head: (0, head)),
            pl.BlockSpec((count, HEAD_DIM), lambda head: (0, head)),
            pl.BlockSpec((count, HEAD_DIM), lambda head: (0, head + kv_local)),
        ],
        out_specs=pl.BlockSpec(wide, lambda head: (0, head)),
        compiler_params=pltpu.CompilerParams(vmem_limit_bytes=40 * 1024 * 1024),
        cost_estimate=pl.CostEstimate(
            flops=4 * rows * count * queries.shape[1],
            bytes_accessed=4 * queries.size + 2 * key_value.size,
            transcendentals=rows * count * kv_local * group_size,
        ),
    )(jnp.stack([limit, first]), queries, key_value, key_value)


def body(
    length,
    residual,
    ssm_input,
    state_in,
    state_out,
    step_raw,
    decay_rate,
    ssm_gain,
    out_weight,
    norm_gain,
    query_weight,
    key_weight,
    value_weight,
):
    rows = residual.shape[0]
    local_heads = decay_rate.shape[0]
    head_width = ssm_input.shape[1] // local_heads
    seq_index = lax.axis_index("seq")
    limit = length[0]
    positions = seq_index * rows + jnp.arange(rows, dtype=jnp.int32)
    live_rows = positions < limit
    live = live_rows.astype(jnp.float32)
    delta = live[None, :] * jax.nn.softplus(step_raw)
    cumlog = jnp.cumsum(-decay_rate[:, None] * delta, axis=1)
    inputs = ssm_input.astype(jnp.float32).reshape(rows, local_heads, head_width)
    inner = jnp.dot(state_out, state_in.T, preferred_element_type=jnp.float32)
    causal = jnp.arange(rows)[:, None] >= jnp.arange(rows)[None, :]
    spread = cumlog[:, :, None] - cumlog[:, None, :]
    mixing = (
        jnp.where(causal[None], jnp.exp(jnp.where(causal[None], spread, 0.0)), 0.0)
        * inner[None]
        * delta[:, None, :]
    )
    within = jnp.einsum("hts,shp->thp", mixing, inputs, precision=HIGHEST)
    tail = jnp.exp(cumlog[:, -1:] - cumlog) * delta
    local_state = jnp.einsum(
        "hs,shp,sn->hpn", tail, inputs, state_in.astype(jnp.float32), precision=HIGHEST
    )
    incoming = incoming_state(jnp.exp(cumlog[:, -1]), local_state, lax.axis_size("seq"))
    carried = jnp.einsum("hpn,tn->thp", incoming, state_out.astype(jnp.float32), precision=HIGHEST)
    ssm_out = (within + jnp.exp(cumlog).T[:, :, None] * carried) * live[:, None, None]
    mean_square = jnp.mean(ssm_out * ssm_out, axis=2, keepdims=True)
    normed = (
        ssm_out * lax.rsqrt(mean_square + EPSILON) * ssm_gain.reshape(local_heads, head_width)
    ).astype(jnp.bfloat16)
    normed = normed.reshape(rows, local_heads * head_width)
    layer_out, queries, key_value = line_layer(
        normed,
        out_weight,
        residual,
        norm_gain,
        (query_weight, key_weight, value_weight),
        lax.axis_size("head"),
        lax.axis_size("seq"),
    )
    head_out = attention(queries, key_value, limit, seq_index * rows)
    return (layer_out, head_out)


def solution(mesh):
    placed = (
        P("doc"),
        P(("doc", "seq"), "head"),
        P(("doc", "seq"), "head"),
        P(("doc", "seq"), None),
        P(("doc", "seq"), None),
        P(("doc", "head"), "seq"),
        P("head"),
        P("head"),
        P("head", None),
        P(),
        P(None, "head"),
        P(None, "head"),
        P(None, "head"),
    )
    return jax.shard_map(
        body,
        mesh=mesh,
        in_specs=placed,
        out_specs=(P(("doc", "seq"), "head"), P(("doc", "seq"), "head")),
        check_vma=False,
    )
```

profile of v0, /device:TPU:0, one launch (start us, length us, event | category | flops | bytes accessed | tf_op | source)
XLA Modules:
  0.0 104.2 jit_solution(832662212234175346)
XLA Ops:
  0.6 0.0 copy-start
  1.3 0.7 neg.8
  2.0 0.1 pad_add_fusion.limits_ref
  2.1 0.8 mul.96
  2.8 0.8 multiply_bitcast_fusion.1
  3.6 0.6 reduce-window.6
  4.2 0.2 slice_reduce_fusion
  4.4 0.1 copy_bitcast_fusion
  4.5 0.2 slice_reduce_fusion.1
  4.6 0.5 exp.19.decay_ref
  5.2 0.1 exponential_bitcast_fusion
  5.3 1.0 fusion.28
  6.3 1.2 %copy.21 = bf16[256,1024]{0,1:T(8,128)(2,1)S(1)} copy(bf16[256,1024]{1,0:T(8,128)(2,1)} %param.15) | data formatting | bytes 1048576 | tf_op args[2]
  7.6 2.3 %fusion.19.state_ref = f32[16,64,128]{2,1,0:T(8,128)} fusion(bf16[256,16,64]{0,2,1:T(8,128)(2,1)S(1)} %bitcast.49, f32[256,16]{0,1:T(8,128)S(1)} %get-tuple-element.11, bf16[256,128]{1,0:T(8,128)(2,1)} %param.16), kind=kOutput, calls=%fused_computation.20 | convolution fusion | flops 403177472 | bytes 1130496 | tf_op jit(solution)/shard_map/hs,shp,sn->hpn/dot_general | solution.py:533
  9.9 3.6 %shard_map.140 = f32[16,64,128]{2,1,0:T(8,128)} custom-call(f32[16]{0:T(128)} %exp.19.decay_ref, f32[16,64,128]{2,1,0:T(8,128)} %fusion.19.state_ref), custom_call_target="tpu_custom_call" | custom-call | tf_op jit(solution)/shard_map/pallas_call | solution.py:88
  13.5 3.4 %fusion.13 = f32[256,16,64]{0,2,1:T(8,128)S(1)} fusion(bf16[256,16,64]{0,2,1:T(8,128)(2,1)S(1)} %bitcast.50, f32[16,256]{1,0:T(8,128)S(1)} %get-tuple-element.9, f32[256,256]{1,0:T(8,128)S(1)} %fusion.28, f32[16,256]{1,0:T(8,128)S(1)} %copy_bitcast_fusion, pred[256,256]{1,0:T(8,128)(4,1)S(1)} %iota_compare_fusion), kind=kOutput, calls=%fused_computation.14 | convolution fusion | flops 810549248 | bytes 1933312 | tf_op jit(solution)/shard_map/hts,shp->thp/dot_general | solution.py:531
  16.9 0.0 copy-start.1
  16.9 0.6 multiply_reduce_fusion
  17.6 0.2 multiply_convert_fusion
  17.8 0.2 copy.22.normed_ref
  18.0 78.3 %shard_map.141 = (bf16[256,1024]{1,0:T(8,128)(2,1)S(1)}, bf16[256,1024]{1,0:T(8,128)(2,1)S(1)}, bf16[1024,512]{1,0:T(8,128)(2,1)}) custom-call(bf16[256,1024]{1,0:T(8,128)(2,1)S(1)} %copy.22.normed_ref, bf16[1024,4096]{1,0:T(8,128)(2,1)} %out_weight_ref.1, bf16[256,1024]{1,0:T(8,128)(2,1)} %residual_ref.1, f32[1,4096]{1,0:T(1,128)S(1)} %bitcast.47, ...), custom_call_target="tpu_custom_call" | custom-call | tf_op jit(solution)/shard_map/pallas_call | solution.py:413
  96.3 1.2 %copy-done.2 = bf16[1024,512]{1,0:T(8,128)(2,1)S(1)} copy-done((bf16[1024,512]{1,0:T(8,128)(2,1)S(1)}, bf16[1024,512]{1,0:T(8,128)(2,1)}, u32[]{:S(2)}) %copy-start.2) | copy-done | bytes 1048600
  97.5 5.9 %shard_map.142 = bf16[256,1024]{1,0:T(8,128)(2,1)} custom-call(s32[2]{0:T(128)S(1)} %pad_add_fusion.limits_ref, bf16[256,1024]{1,0:T(8,128)(2,1)S(1)} %get-tuple-element.6.query_ref, bf16[1024,512]{1,0:T(8,128)(2,1)S(1)} %copy-done.2, bf16[1024,512]{1,0:T(8,128)(2,1)S(1)} %copy-done.2), custom_call_target="tpu_custom_call" | custom-call | flops 1073741824 | bytes 2097152 | tf_op jit(solution)/shard_map/pallas_call | solution.py:477
  103.4 0.8 copy.34
  (11 shorter events, 0.1 us)
Async XLA Ops:
  0.6 4.7 %copy-start = (bf16[256,128]{1,0:T(8,128)(2,1)S(1)}, bf16[256,128]{1,0:T(8,128)(2,1)}, u32[]{:S(2)}) copy-start(bf16[256,128]{1,0:T(8,128)(2,1)} %param.17) | copy-start | bytes 196612
  13.5 3.4 %copy-start.3 = (f32[16,64,128]{2,1,0:T(8,128)S(1)}, f32[16,64,128]{2,1,0:T(8,128)}, u32[]{:S(2)}) copy-start(f32[16,64,128]{2,1,0:T(8,128)} %shard_map.140) | copy-start | bytes 1572868
  16.9 1.1 %copy-start.1 = (f32[4096]{0:T(1024)S(1)}, f32[4096]{0:T(1024)}, u32[]{:S(2)}) copy-start(f32[4096]{0:T(1024)} %param.22) | copy-start | bytes 49156
  96.3 1.2 %copy-start.2 = (bf16[1024,512]{1,0:T(8,128)(2,1)S(1)}, bf16[1024,512]{1,0:T(8,128)(2,1)}, u32[]{:S(2)}) copy-start(bf16[1024,512]{1,0:T(8,128)(2,1)} %get-tuple-element.7.key_ref.value_ref) | copy-start | bytes 3145732
where the time goes:
time: 105 us; the launch traced here: 104 us
  Pallas kernels  87.8 us (84%)
  matrix products  7.34 us (7%)
  local copies, waits for them, and re-layouts  5.12 us (5%)
  other arithmetic  2.52 us (2%)
  between operations  1.45 us (1%)
    pallas_call x1, Pallas kernels, line_layer(): pl.pallas_call(functools.partial(line_kernel, count, shards, chunks), out...  78.3 us
    pallas_call x1, Pallas kernels, attention(): pl.pallas_call(functools.partial(attention_kernel, group_size), grid=(kv_...  5.93 us
    pallas_call x1, Pallas kernels, incoming_state(): pl.pallas_call(functools.partial(chain_kernel, count, chunks), out_shape=...  3.61 us
    dot_general x1, matrix products, body(): within = jnp.einsum('hts,shp->thp', mixing, inputs, precision=HIGHEST)  3.38 us
    unnamed x10, local copies, waits for them, and re-layouts  3.28 us
    dot_general x1, matrix products, body(): jnp.einsum('hs,shp,sn->hpn', tail, inputs, state_in.astype(jnp.float32),...  2.29 us

commit v1 on v0

--- a/solution.py
+++ b/solution.py
@@ -107,6 +107,7 @@
     count,
     shards,
     chunks,
+    lag,
     normed_ref,
     out_weight_ref,
     residual_ref,
@@ -124,12 +125,11 @@
     shared_ref,
     stage_ref,
     landed_ref,
-    gathered_ref,
-    total_ref,
+    final_ref,
     sum_send,
     sum_recv,
-    copy_send,
-    copy_recv,
+    final_send,
+    final_recv,
     shard_send,
     shard_recv,
     weight_sem,
@@ -137,14 +137,24 @@
 ):
     mine = lax.axis_index("head")
     last = count - 1
-    width = residual_ref.shape[1]
-    rows = residual_ref.shape[0] // chunks
-    place = (mine, last - mine)
+    half = count // 2
+    left = mine < half
+    place = jnp.where(left, mine, last - mine)
+    inner = (mine == half - 1) | (mine == half)
+    inward = jnp.where(left, mine + 1, mine - 1)
+    outward = jnp.where(left, mine - 1, mine + 1)
+    inner_slot = inner.astype(jnp.int32)
+
+    pieces, piece_rows, piece_width = stage_ref.shape
+    rows, width = residual_ref.shape
+    blocks = pieces // chunks
+    per_owner = width // piece_width
 
     shard = lax.axis_index("seq")
     query_width = query_ref.shape[1]
     kv_width = key_weight_ref.shape[1]
-    starts = (0, kv_width, 2 * kv_width)
+    tile = 2 * kv_width
+    starts = (0, kv_width, tile)
     loads = [
         pltpu.make_async_copy(
             source, weight_ref.at[:, pl.ds(start, source.shape[1])], weight_sem.at[index]
@@ -154,32 +164,18 @@
         )
     ]
 
-    def ordered(index):
-        return jnp.where(2 * mine < count, last - index, index)
-
-    def block_load(index):
-        columns = pl.ds(pl.multiple_of(ordered(index) * width, 128), width)
+    def block_load(block):
+        columns = pl.ds(pl.multiple_of(block * piece_width, 128), piece_width)
         return pltpu.make_async_copy(
-            out_weight_ref.at[:, columns], block_weight_ref.at[index], block_sem.at[index]
-        )
-
-    for index in range(count):
-        block_load(index).start()
+            out_weight_ref.at[:, columns], block_weight_ref.at[block], block_sem.at[block]
+        )
+
+    @pl.loop(0, blocks)
+    def _(block):
+        block_load(block).start()
+
     for load in loads:
         load.start()
-
-    def compute_block(index):
-        block_load(index).wait()
-        tile = min(width, 256)
-
-        @pl.loop(0, width // tile)
-        def _(step):
-            columns = pl.ds(pl.multiple_of(step * tile, 128), tile)
-            partial_ref[ordered(index), :, columns] = jnp.dot(
-                normed_ref[...],
-                block_weight_ref[index, :, columns],
-                preferred_element_type=jnp.float32,
-            )
 
     barrier = pltpu.get_barrier_semaphore()
 
@@ -210,44 +206,29 @@
     def _():
         pl.semaphore_wait(barrier, shards + 1)
 
-    for other in range(shards):
-
-        @pl.when(other > shard)
-        def _():
-            shared_ref[pl.ds(other * residual_ref.shape[0], residual_ref.shape[0])] = jnp.zeros(
-                (residual_ref.shape[0], 2 * kv_width), jnp.bfloat16
-            )
-
-    def neighbour(way):
-        return mine + 1 if way == 0 else mine - 1
-
-    def real(way, position):
-        return position if way == 0 else last - position
-
-    def sum_copy(way, chunk, step):
+    def sum_copy(piece, slot):
         return pltpu.make_async_remote_copy(
-            src_ref=stage_ref.at[way, chunk, step],
-            dst_ref=landed_ref.at[way, chunk, step],
-            send_sem=sum_send.at[way, chunk, step],
-            recv_sem=sum_recv.at[way, chunk, step],
-            device_id={"head": neighbour(way)},
+            src_ref=stage_ref.at[piece],
+            dst_ref=landed_ref.at[slot, piece],
+            send_sem=sum_send.at[piece],
+            recv_sem=sum_recv.at[slot, piece],
+            device_id={"head": inward},
             device_id_type=pl.DeviceIdType.MESH,
         )
 
-    def block_copy(way, chunk, step, source):
-        block = gathered_ref.at[source, pl.ds(chunk * rows, rows)]
+    def final_copy(piece):
         return pltpu.make_async_remote_copy(
-            src_ref=block,
-            dst_ref=block,
-            send_sem=copy_send.at[way, chunk, step],
-            recv_sem=copy_recv.at[way, chunk, step],
-            device_id={"head": neighbour(way)},
+            src_ref=final_ref.at[piece],
+            dst_ref=final_ref.at[piece],
+            send_sem=final_send.at[piece],
+            recv_sem=final_recv.at[piece],
+            device_id={"head": outward},
             device_id_type=pl.DeviceIdType.MESH,
         )
 
     def shard_copy(chunk, offset, source):
-        start = pl.multiple_of(source * residual_ref.shape[0] + chunk * rows, 16)
-        block = shared_ref.at[pl.ds(start, rows)]
+        start = pl.multiple_of(source * rows + chunk * piece_rows, 16)
+        block = shared_ref.at[pl.ds(start, piece_rows)]
         return pltpu.make_async_remote_copy(
             src_ref=block,
             dst_ref=block,
@@ -257,137 +238,153 @@
             device_id_type=pl.DeviceIdType.MESH,
         )
 
-    def project(chunk):
-        here = pl.ds(chunk * rows, rows)
-        there = pl.ds(pl.multiple_of(shard * residual_ref.shape[0] + chunk * rows, 16), rows)
-
-        def product(tile):
-            columns = pl.ds(pl.multiple_of(tile * kv_width, 128), kv_width)
-            return jnp.dot(
-                attn_ref[here], weight_ref[:, columns], preferred_element_type=jnp.float32
+    def chunk_rows(chunk):
+        return pl.ds(pl.multiple_of(chunk * piece_rows, 16), piece_rows)
+
+    def compute(block):
+        products = jnp.dot(
+            normed_ref[...], block_weight_ref[block], preferred_element_type=jnp.float32
+        )
+        for chunk in range(chunks):
+            here = slice(chunk * piece_rows, (chunk + 1) * piece_rows)
+            partial_ref[chunk * blocks + block] = products[here]
+
+        @pl.when(block // per_owner == mine)
+        def _():
+            columns = pl.ds(
+                pl.multiple_of((block % per_owner) * piece_width, 128), piece_width
+            )
+            for chunk in range(chunks):
+                here = slice(chunk * piece_rows, (chunk + 1) * piece_rows)
+                partial_ref[chunk * blocks + block] += residual_ref[here, columns].astype(
+                    jnp.float32
+                )
+
+        @pl.when(place == 0)
+        def _():
+            for chunk in range(chunks):
+                piece = chunk * blocks + block
+                stage_ref[piece] = partial_ref[piece].astype(jnp.bfloat16)
+            sum_copy(block, inner_slot).start()
+
+    def pass_inward(piece):
+        @pl.when(place > 0)
+        def _():
+            sum_copy(piece, 0).wait_recv()
+            arrived = landed_ref[0, piece].astype(jnp.float32)
+            stage_ref[piece] = (partial_ref[piece] + arrived).astype(jnp.bfloat16)
+            sum_copy(piece, inner_slot).start()
+
+    def finish(piece):
+        @pl.when(inner)
+        def _():
+            sum_copy(piece, 1).wait_recv()
+            final_ref[piece] = (
+                stage_ref[piece].astype(jnp.float32) + landed_ref[1, piece].astype(jnp.float32)
             ).astype(jnp.bfloat16)
 
-        if chunk == 0:
-            for load in loads:
-                load.wait()
-
-        @pl.loop(0, 2)
-        def _(tile):
-            columns = pl.ds(pl.multiple_of(tile * kv_width, 128), kv_width)
-            shared_ref[there, columns] = product(tile)
-
+        @pl.when(jnp.logical_not(inner))
+        def _():
+            final_copy(piece).wait_recv()
+
+        @pl.when(place > 0)
+        def _():
+            final_copy(piece).start()
+
+    def normalise(chunk):
+        squares = jnp.zeros((piece_rows, 1), jnp.float32)
+        for block in range(blocks):
+            values = final_ref[chunk * blocks + block].astype(jnp.float32)
+            squares += jnp.sum(values * values, axis=1, keepdims=True)
+        scale = lax.rsqrt(squares / (count * width) + EPSILON)
+        for block in range(blocks):
+            columns = slice(block * piece_width, (block + 1) * piece_width)
+            values = final_ref[chunk * blocks + block].astype(jnp.float32)
+            attn_ref[:, columns] = (values * scale * gain_ref[:, columns]).astype(jnp.bfloat16)
+        for part in range(per_owner):
+            columns = slice(part * piece_width, (part + 1) * piece_width)
+            layer_ref[chunk_rows(chunk), columns] = final_ref[
+                chunk * blocks + mine * per_owner + part
+            ]
+
+    def product(index):
+        columns = pl.ds(pl.multiple_of(index * tile, 128), tile)
+        return jnp.dot(
+            attn_ref[...], weight_ref[:, columns], preferred_element_type=jnp.float32
+        ).astype(jnp.bfloat16)
+
+    def project_shared(chunk):
+        start = pl.multiple_of(shard * rows + chunk * piece_rows, 16)
+        shared_ref[pl.ds(start, piece_rows)] = product(0)
         for offset in range(1, shards):
 
             @pl.when(shard + offset < shards)
             def _():
                 shard_copy(chunk, offset, shard).start()
 
-        @pl.loop(0, query_width // kv_width)
-        def _(tile):
-            columns = pl.ds(pl.multiple_of(tile * kv_width, 128), kv_width)
-            query_ref[here, columns] = product(tile + 2)
-
-    def own_part(chunk, owner):
-        return partial_ref[owner, pl.ds(chunk * rows, rows)]
-
-    def sum_step(chunk, step):
-        for way in range(2):
-            owner = real(way, last - step + place[way])
-
-            @pl.when(place[way] == 0)
+    def project_query(chunk, index):
+        columns = pl.ds(pl.multiple_of(index * tile, 128), tile)
+        query_ref[chunk_rows(chunk), columns] = product(index + 1)
+
+    @pl.loop(0, blocks)
+    def _(block):
+        block_load(block).wait()
+        compute(block)
+
+    @pl.when(place == 0)
+    def _():
+        @pl.loop(blocks, pieces)
+        def _(piece):
+            sum_copy(piece, inner_slot).start()
+
+    for other in range(shards):
+
+        @pl.when(other > shard)
+        def _():
+            shared_ref[pl.ds(other * rows, rows)] = jnp.zeros((rows, tile), jnp.bfloat16)
+
+    query_tiles = query_width // tile
+    spacing = max(1, (blocks - 1) // (1 + query_tiles))
+    first = lag + blocks - 1
+
+    @pl.loop(0, pieces + lag + blocks - 1)
+    def _(tick):
+        @pl.when(tick < pieces)
+        def _():
+            pass_inward(tick)
+
+        @pl.when((tick >= lag) & (tick < pieces + lag))
+        def _():
+            finish(tick - lag)
+
+        @pl.when(tick == first)
+        def _():
+            for load in loads:
+                load.wait()
+
+        @pl.when(tick >= first)
+        def _():
+            chunk, turn = (tick - first) // blocks, (tick - first) % blocks
+
+            @pl.when(turn == 0)
             def _():
-                stage_ref[way, chunk, step] = own_part(chunk, owner).astype(jnp.bfloat16)
-                sum_copy(way, chunk, step).start()
-
-            if step == 0:
-                continue
-
-            @pl.when((place[way] <= step) & (place[way] > 0))
+                normalise(chunk)
+                project_shared(chunk)
+
+            @pl.when((turn > 0) & (turn % spacing == 0) & (turn // spacing <= query_tiles))
             def _():
-                sum_copy(way, chunk, step - 1).wait_recv()
-                arrived = landed_ref[way, chunk, step - 1].astype(jnp.float32)
-                stage_ref[way, chunk, step] = (own_part(chunk, owner) + arrived).astype(
-                    jnp.bfloat16
-                )
-                sum_copy(way, chunk, step).start()
-
-    def finish_sum(chunk):
-        here = pl.ds(chunk * rows, rows)
-        total_ref[...] = residual_ref[here].astype(jnp.float32) + own_part(chunk, mine)
-        for way in range(2):
-
-            @pl.when(place[way] > 0)
-            def _():
-                sum_copy(way, chunk, last - 1).wait_recv()
-                total_ref[...] += landed_ref[way, chunk, last - 1].astype(jnp.float32)
-
-        layer_low = total_ref[...].astype(jnp.bfloat16)
-        gathered_ref[mine, here] = layer_low
-        layer_ref[here] = layer_low
-        for way in range(2):
-
-            @pl.when(place[way] < last)
-            def _():
-                block_copy(way, chunk, 0, mine).start()
-
-    def forward(chunk, step):
-        for way in range(2):
-            source = real(way, place[way] - step)
-
-            @pl.when(place[way] >= step)
-            def _():
-                block_copy(way, chunk, step - 1, source).wait_recv()
-
-            @pl.when((place[way] >= step) & (place[way] < last))
-            def _():
-                block_copy(way, chunk, step, source).start()
-
-    def normalise(chunk):
-        for way in range(2):
-
-            @pl.when(place[way] == last)
-            def _():
-                block_copy(way, chunk, last - 1, real(way, 0)).wait_recv()
-
-        here = pl.ds(chunk * rows, rows)
-        squares = jnp.zeros((rows, 1), jnp.float32)
-        for source in range(count):
-            block = gathered_ref[source, here].astype(jnp.float32)
-            squares += jnp.sum(block * block, axis=1, keepdims=True)
-        scale = lax.rsqrt(squares / (count * width) + EPSILON)
-        for source in range(count):
-            columns = slice(source * width, (source + 1) * width)
-            block = gathered_ref[source, here].astype(jnp.float32)
-            attn_ref[here, columns] = (block * scale * gain_ref[:, columns]).astype(jnp.bfloat16)
-
-    for tick in range(chunks + 2 * last):
-        for index in range(count) if tick < 3 else ():
-            if min(index, 2) == tick:
-                compute_block(index)
-        for chunk in range(chunks):
-            stage = tick - chunk
-            if 0 <= stage < last:
-                sum_step(chunk, stage)
-            elif stage == last:
-                finish_sum(chunk)
-            elif last < stage < 2 * last:
-                forward(chunk, stage - last)
-        if 0 <= tick - 2 * last < chunks:
-            normalise(tick - 2 * last)
-            project(tick - 2 * last)
-
-    for chunk in range(chunks):
-        for step in range(last):
-            for way in range(2):
-
-                @pl.when(place[way] <= step)
-                def _():
-                    sum_copy(way, chunk, step).wait_send()
-
-                @pl.when((place[way] >= step) & (place[way] < last))
-                def _():
-                    block_copy(way, chunk, step, real(way, place[way] - step)).wait_send()
-
+                project_query(chunk, turn // spacing - 1)
+
+    @pl.loop(0, pieces)
+    def _(piece):
+        sum_copy(piece, inner_slot).wait_send()
+
+        @pl.when(place > 0)
+        def _():
+            final_copy(piece).wait_send()
+
+    @pl.loop(0, chunks)
+    def _(chunk):
         for offset in range(1, shards):
 
             @pl.when(shard + offset < shards)
@@ -405,13 +402,16 @@
     rows, width = residual.shape
     model_width = width * count
     query_width, kv_width = weights[0].shape[1], weights[1].shape[1]
-    chunks = 4 if rows % 64 == 0 else 1
-    piece = rows // chunks
-    messages = (2, chunks, count - 1)
+    piece_rows = 64 if rows % 64 == 0 else rows
+    piece_width = 512 if width % 512 == 0 else width
+    chunks, blocks = rows // piece_rows, model_width // piece_width
+    pieces = chunks * blocks
+    piece = (piece_rows, piece_width)
+    lag = 3 * max(1, count - 3)
     vmem = pl.BlockSpec(memory_space=pltpu.VMEM)
     hbm = pl.BlockSpec(memory_space=pltpu.HBM)
     return pl.pallas_call(
-        functools.partial(line_kernel, count, shards, chunks),
+        functools.partial(line_kernel, count, shards, chunks, lag),
         out_shape=(
             jax.ShapeDtypeStruct((rows, width), jnp.bfloat16),
             jax.ShapeDtypeStruct((rows, query_width), jnp.bfloat16),
@@ -420,23 +420,22 @@
         in_specs=[vmem, hbm, vmem, vmem, hbm, hbm, hbm],
         out_specs=[vmem] * 3,
         scratch_shapes=[
-            pltpu.VMEM((count, out_weight.shape[0], width), jnp.bfloat16),
-            pltpu.VMEM((count, rows, width), jnp.float32),
+            pltpu.VMEM((blocks, out_weight.shape[0], piece_width), jnp.bfloat16),
+            pltpu.VMEM((pieces,) + piece, jnp.float32),
             pltpu.VMEM((model_width, 2 * kv_width + query_width), jnp.bfloat16),
-            pltpu.VMEM((rows, model_width), jnp.bfloat16),
+            pltpu.VMEM((piece_rows, model_width), jnp.bfloat16),
             pltpu.VMEM((shards * rows, 2 * kv_width), jnp.bfloat16),
-            pltpu.VMEM(messages + (piece, width), jnp.bfloat16),
-            pltpu.VMEM(messages + (piece, width), jnp.bfloat16),
-            pltpu.VMEM((count, rows, width), jnp.bfloat16),
-            pltpu.VMEM((piece, width), jnp.float32),
-            pltpu.SemaphoreType.DMA(messages),
-            pltpu.SemaphoreType.DMA(messages),
-            pltpu.SemaphoreType.DMA(messages),
-            pltpu.SemaphoreType.DMA(messages),
+            pltpu.VMEM((pieces,) + piece, jnp.bfloat16),
+            pltpu.VMEM((2, pieces) + piece, jnp.bfloat16),
+            pltpu.VMEM((pieces,) + piece, jnp.bfloat16),
+            pltpu.SemaphoreType.DMA((pieces,)),
+            pltpu.SemaphoreType.DMA((2, pieces)),
+            pltpu.SemaphoreType.DMA((pieces,)),
+            pltpu.SemaphoreType.DMA((pieces,)),
             pltpu.SemaphoreType.DMA((chunks, shards)),
             pltpu.SemaphoreType.DMA((chunks, shards)),
             pltpu.SemaphoreType.DMA((3,)),
-            pltpu.SemaphoreType.DMA((count,)),
+            pltpu.SemaphoreType.DMA((blocks,)),
         ],
         compiler_params=pltpu.CompilerParams(
             collective_id=0, has_side_effects=True, vmem_limit_bytes=52 * 1024 * 1024

time: 105 us -> 97.9 us (0.932)
  Pallas kernels: 87.8 us -> 80.9 us
    pallas_call x1, Pallas kernels: 78.3 us -> 71.4 us  [line_layer(): pl.pallas_call(functools.partial(line_kernel, count, shards, chunks, lag)...]
where the time goes in v1:
time: 97.9 us; the launch traced here: 97.4 us
  Pallas kernels  80.9 us (83%)
  matrix products  7.33 us (7%)
  local copies, waits for them, and re-layouts  5.12 us (5%)
  other arithmetic  2.52 us (3%)
  between operations  1.45 us (1%)
    pallas_call x1, Pallas kernels, line_layer(): pl.pallas_call(functools.partial(line_kernel, count, shards, chunks, lag)...  71.4 us
    pallas_call x1, Pallas kernels, attention(): pl.pallas_call(functools.partial(attention_kernel, group_size), grid=(kv_...  5.94 us
    pallas_call x1, Pallas kernels, incoming_state(): pl.pallas_call(functools.partial(chain_kernel, count, chunks), out_shape=...  3.61 us
    dot_general x1, matrix products, body(): within = jnp.einsum('hts,shp->thp', mixing, inputs, precision=HIGHEST)  3.37 us
    unnamed x10, local copies, waits for them, and re-layouts  3.28 us
    dot_general x1, matrix products, body(): jnp.einsum('hs,shp,sn->hpn', tail, inputs, state_in.astype(jnp.float32),...  2.29 us

profile of v1, /device:TPU:0, one launch (start us, length us, event | category | flops | bytes accessed | tf_op | source)
XLA Modules:
  0.0 97.4 jit_solution(2733757162550471415)
XLA Ops:
  0.6 0.0 copy-start
  1.3 0.7 neg.8
  2.0 0.1 pad_add_fusion.limits_ref
  2.1 0.8 mul.96
  2.8 0.8 multiply_bitcast_fusion.1
  3.6 0.6 reduce-window.6
  4.2 0.2 slice_reduce_fusion
  4.4 0.1 copy_bitcast_fusion
  4.5 0.2 slice_reduce_fusion.1
  4.6 0.5 exp.19.decay_ref
  5.2 0.1 exponential_bitcast_fusion
  5.3 1.0 %fusion.28 = f32[256,256]{1,0:T(8,128)S(1)} fusion(bf16[256,128]{1,0:T(8,128)(2,1)S(1)} %copy-done, bf16[256,128]{1,0:T(8,128)(2,1)} %param.16), kind=kOutput, calls=%fused_computation.41 | convolution fusion | flops 16777216 | bytes 393216 | tf_op jit(solution)/shard_map/dot_general | solution.py:522
  6.3 1.2 %copy.21 = bf16[256,1024]{0,1:T(8,128)(2,1)S(1)} copy(bf16[256,1024]{1,0:T(8,128)(2,1)} %param.15) | data formatting | bytes 1048576 | tf_op args[2]
  7.6 2.3 %fusion.19.state_ref = f32[16,64,128]{2,1,0:T(8,128)} fusion(bf16[256,16,64]{0,2,1:T(8,128)(2,1)S(1)} %bitcast.49, f32[256,16]{0,1:T(8,128)S(1)} %get-tuple-element.11, bf16[256,128]{1,0:T(8,128)(2,1)} %param.16), kind=kOutput, calls=%fused_computation.20 | convolution fusion | flops 403177472 | bytes 1130496 | tf_op jit(solution)/shard_map/hs,shp,sn->hpn/dot_general | solution.py:532
  9.9 3.6 %shard_map.140 = f32[16,64,128]{2,1,0:T(8,128)} custom-call(f32[16]{0:T(128)} %exp.19.decay_ref, f32[16,64,128]{2,1,0:T(8,128)} %fusion.19.state_ref), custom_call_target="tpu_custom_call" | custom-call | tf_op jit(solution)/shard_map/pallas_call | solution.py:88
  13.5 3.4 %fusion.13 = f32[256,16,64]{0,2,1:T(8,128)S(1)} fusion(bf16[256,16,64]{0,2,1:T(8,128)(2,1)S(1)} %bitcast.50, f32[16,256]{1,0:T(8,128)S(1)} %get-tuple-element.9, f32[256,256]{1,0:T(8,128)S(1)} %fusion.28, f32[16,256]{1,0:T(8,128)S(1)} %copy_bitcast_fusion, pred[256,256]{1,0:T(8,128)(4,1)S(1)} %iota_compare_fusion), kind=kOutput, calls=%fused_computation.14 | convolution fusion | flops 810549248 | bytes 1933312 | tf_op jit(solution)/shard_map/hts,shp->thp/dot_general | solution.py:530
  16.9 0.0 copy-start.1
  16.9 0.6 multiply_reduce_fusion
  17.6 0.2 multiply_convert_fusion
  17.8 0.2 copy.22.normed_ref
  18.0 71.4 %shard_map.141 = (bf16[256,1024]{1,0:T(8,128)(2,1)S(1)}, bf16[256,1024]{1,0:T(8,128)(2,1)S(1)}, bf16[1024,512]{1,0:T(8,128)(2,1)}) custom-call(bf16[256,1024]{1,0:T(8,128)(2,1)S(1)} %copy.22.normed_ref, bf16[1024,4096]{1,0:T(8,128)(2,1)} %out_weight_ref.1, bf16[256,1024]{1,0:T(8,128)(2,1)} %residual_ref.1, f32[1,4096]{1,0:T(1,128)S(1)} %bitcast.47, ...), custom_call_target="tpu_custom_call" | custom-call | tf_op jit(solution)/shard_map/pallas_call | solution.py:413
  89.4 1.2 %copy-done.2 = bf16[1024,512]{1,0:T(8,128)(2,1)S(1)} copy-done((bf16[1024,512]{1,0:T(8,128)(2,1)S(1)}, bf16[1024,512]{1,0:T(8,128)(2,1)}, u32[]{:S(2)}) %copy-start.2) | copy-done | bytes 1048600
  90.6 5.9 %shard_map.142 = bf16[256,1024]{1,0:T(8,128)(2,1)} custom-call(s32[2]{0:T(128)S(1)} %pad_add_fusion.limits_ref, bf16[256,1024]{1,0:T(8,128)(2,1)S(1)} %get-tuple-element.6.query_ref, bf16[1024,512]{1,0:T(8,128)(2,1)S(1)} %copy-done.2, bf16[1024,512]{1,0:T(8,128)(2,1)S(1)} %copy-done.2), custom_call_target="tpu_custom_call" | custom-call | flops 1073741824 | bytes 2097152 | tf_op jit(solution)/shard_map/pallas_call | solution.py:476
  96.6 0.8 copy.34
  (11 shorter events, 0.1 us)
Async XLA Ops:
  0.6 4.7 %copy-start = (bf16[256,128]{1,0:T(8,128)(2,1)S(1)}, bf16[256,128]{1,0:T(8,128)(2,1)}, u32[]{:S(2)}) copy-start(bf16[256,128]{1,0:T(8,128)(2,1)} %param.17) | copy-start | bytes 196612
  13.5 3.4 %copy-start.3 = (f32[16,64,128]{2,1,0:T(8,128)S(1)}, f32[16,64,128]{2,1,0:T(8,128)}, u32[]{:S(2)}) copy-start(f32[16,64,128]{2,1,0:T(8,128)} %shard_map.140) | copy-start | bytes 1572868
  16.9 1.1 %copy-start.1 = (f32[4096]{0:T(1024)S(1)}, f32[4096]{0:T(1024)}, u32[]{:S(2)}) copy-start(f32[4096]{0:T(1024)} %param.22) | copy-start | bytes 49156
  89.4 1.2 %copy-start.2 = (bf16[1024,512]{1,0:T(8,128)(2,1)S(1)}, bf16[1024,512]{1,0:T(8,128)(2,1)}, u32[]{:S(2)}) copy-start(bf16[1024,512]{1,0:T(8,128)(2,1)} %get-tuple-element.7.key_ref.value_ref) | copy-start | bytes 3145732
